TPU v7x, 32 devices: a whole 2x2x4 slice. The times are simulated.
32 devices in a mesh: shard: 4 (over z), width: 2 (over core), shift: 4 (over y, x).
Axes of the slice: x: 2, y: 2, z: 4, core: 2. Of those that a mesh axis runs over, the one named last changes fastest.
Arguments:
- w_query: bfloat16 [8192, 2048], P(('shift', 'shard'), 'width'), parts along dimension 0, may hold values from -0.125 to 0.125
- low_query: bfloat16 [8192, 16], P(('shift', 'shard')), parts along dimension 0, may hold values from -0.125 to 0.125
- high_query: bfloat16 [64, 2048], P('shift', 'width'), parts along dimension 0, may hold values from -1.5 to 1.5
- w_key: bfloat16 [8192, 512], P(('shift', 'shard'), 'width'), parts along dimension 0, may hold values from -0.125 to 0.125
- low_key: bfloat16 [8192, 16], P(('shift', 'shard')), parts along dimension 0, may hold values from -0.125 to 0.125
- high_key: bfloat16 [64, 512], P('shift', 'width'), parts along dimension 0, may hold values from -1.5 to 1.5
- w_value: bfloat16 [8192, 512], P(('shift', 'shard'), 'width'), parts along dimension 0, may hold values from -0.125 to 0.125
- low_value: bfloat16 [8192, 16], P(('shift', 'shard')), parts along dimension 0, may hold values from -0.125 to 0.125
- high_value: bfloat16 [64, 512], P('shift', 'width'), parts along dimension 0, may hold values from -1.5 to 1.5
- w_mixed: bfloat16 [8192, 2048], P(('shift', 'width'), 'shard'), parts along dimension 0, may hold values from -0.125 to 0.125
- low_mixed: bfloat16 [8192, 16], P(('shift', 'width')), parts along dimension 0, may hold values from -0.125 to 0.125
- high_mixed: bfloat16 [64, 2048], P('shift', 'shard'), parts along dimension 0, may hold values from -1.5 to 1.5
- norm_train: float32 [8192], P(('shift', 'shard', 'width')), parts along dimension 0, may hold values from 0.25 to 1.75
- norm_step: float32 [8192], P(('shift', 'shard', 'width')), parts along dimension 0, may hold values from -0.3 to 0.3
Outputs:
- final_query: bfloat16 [8192, 2048], P(('shift', 'width')), parts along dimension 0
- final_key: bfloat16 [2048, 2048], P(('shift', 'width')), parts along dimension 0
- final_value: bfloat16 [2048, 2048], P(('shift', 'width')), parts along dimension 0
- final_mixed: bfloat16 [8192, 2048], P('shift', 'width'), parts along dimension 0
- serve_norm: bfloat16 [8192], P('shift'), parts along dimension 0
There are 4 independent parts, one for each index of `shift`. A program takes and returns all parts, laid end to end along the dimension named above; each array names one. Nothing has to cross between parts.
All inputs are finite; a program needn't handle non-finite values.
Results may differ from a plain program's by a relative error of at most 0.001.
Values may be sent and summed in bfloat16 or wider, within the bound.
A program may use at most 64 MiB of HBM per device.

v0:
```python
import jax
import jax.numpy as jnp
from jax import lax
from jax.sharding import PartitionSpec as P

mix_rate = 0.5


def on_device(
    w_query,
    low_query,
    high_query,
    w_key,
    low_key,
    high_key,
    w_value,
    low_value,
    high_value,
    w_mixed,
    low_mixed,
    high_mixed,
    norm_train,
    norm_step,
):
    result_query = w_query.astype(jnp.float32) + mix_rate * jnp.dot(
        low_query, high_query, preferred_element_type=jnp.float32
    )
    result_key = w_key.astype(jnp.float32) + mix_rate * jnp.dot(
        low_key, high_key, preferred_element_type=jnp.float32
    )
    result_value = w_value.astype(jnp.float32) + mix_rate * jnp.dot(
        low_value, high_value, preferred_element_type=jnp.float32
    )
    result_mixed = w_mixed.astype(jnp.float32) + mix_rate * jnp.dot(
        low_mixed, high_mixed, preferred_element_type=jnp.float32
    )
    narrow_query, narrow_key, narrow_value, narrow_mixed = (
        result_query.astype(jnp.bfloat16),
        result_key.astype(jnp.bfloat16),
        result_value.astype(jnp.bfloat16),
        result_mixed.astype(jnp.bfloat16),
    )
    final_query, final_key, final_value, final_mixed = (
        lax.all_gather(narrow_query, "shard", axis=0, tiled=True),
        lax.all_gather(narrow_key, "shard", axis=0, tiled=True),
        lax.all_gather(narrow_value, "shard", axis=0, tiled=True),
        lax.all_gather(narrow_mixed, "shard", axis=1, tiled=True),
    )
    final_query, final_key, final_value, final_mixed = (
        final_query.T,
        final_key.T,
        final_value.T,
        final_mixed.T,
    )
    serve_norm = lax.all_gather(
        (norm_train + norm_step).astype(jnp.bfloat16), ("shard", "width"), axis=0, tiled=True
    )
    return (final_query, final_key, final_value, final_mixed, serve_norm)


def solution(mesh):
    placed = (
        P(("shift", "shard"), "width"),
        P(("shift", "shard"), None),
        P("shift", "width"),
        P(("shift", "shard"), "width"),
        P(("shift", "shard"), None),
        P("shift", "width"),
        P(("shift", "shard"), "width"),
        P(("shift", "shard"), None),
        P("shift", "width"),
        P(("shift", "width"), "shard"),
        P(("shift", "width"), None),
        P("shift", "shard"),
        P(("shift", "shard", "width")),
        P(("shift", "shard", "width")),
    )
    return jax.shard_map(
        on_device,
        mesh=mesh,
        in_specs=placed,
        out_specs=(
            P(("shift", "width"), None),
            P(("shift", "width"), None),
            P(("shift", "width"), None),
            P("shift", "width"),
            P("shift"),
        ),
        check_vma=False,
    )
```

profile of v0, /device:TPU:0, one launch (start us, length us, event | category | flops | bytes accessed | tf_op | source)
XLA Modules:
  0.0 246.3 jit_solution(7538486421135906362)
XLA Ops:
  7.2 0.0 copy-start
  7.2 0.0 all-gather.8.cloned.1.call-start
  7.2 1.9 fusion.3
  9.2 0.0 all-gather.8.cloned.1.call-update
  9.2 0.0 all-gather.10.cloned.1.call-start
  9.3 2.0 fusion.2
  11.3 0.0 all-gather.10.cloned.1.call-update
  11.3 0.0 all-gather.6.cloned.1.call-start
  11.4 0.0 copy-done
  11.4 2.7 %add_convert_fusion.1 = bf16[512,1024]{1,0:T(8,128)(2,1)} fusion(bf16[512,1024]{1,0:T(8,128)(2,1)} %param.14, bf16[512,16]{0,1:T(8,128)(2,1)} %param.15, bf16[16,1024]{1,0:T(8,128)(2,1)S(1)} %copy-done), kind=kOutput, calls=%fused_computation.1 | convolution fusion | flops 18874368 | bytes 2146304 | tf_op jit(solution)/shard_map/dot_general | solution.py:25
  14.0 0.0 all-gather.6.cloned.1.call-update
  14.1 0.0 all-gather.12.cloned.1.call-start
  14.1 1.4 add_convert_fusion
  15.6 0.0 all-gather.12.cloned.1.call-update
  15.7 13.7 %all-gather = bf16[8,1,256]{2,1,0:T(2,128)(2,1)S(1)} all-gather(bf16[1,1,256]{2,1,0:T(2,128)(2,1)S(1)} %reshape.10), channel_id=1, replica_groups=mesh['shard'=4,'width'=2,'shift'=4] {'shard','width'}, dimensions={0}, use_global_device_ids=true | all-gather | bytes 4608 | tf_op jit(solution)/shard_map/all_gather | solution.py:55
  29.4 0.6 copy.31
  30.0 10.9 %all-gather.8.cloned.1.call-done = bf16[2048,256]{1,0:T(8,128)(2,1)} async-done(((bf16[512,256]{1,0:T(8,128)(2,1)}), bf16[2048,256]{1,0:T(8,128)(2,1)}) %all-gather.8.cloned.1.call-update) | async-done | bytes 1048592 | tf_op jit(solution)/shard_map/all_gather | solution.py:45
  40.9 2.3 copy.28
  43.2 27.3 %all-gather.10.cloned.1.call-done = bf16[2048,256]{1,0:T(8,128)(2,1)} async-done(((bf16[512,256]{1,0:T(8,128)(2,1)}), bf16[2048,256]{1,0:T(8,128)(2,1)}) %all-gather.10.cloned.1.call-update) | async-done | bytes 1048592 | tf_op jit(solution)/shard_map/all_gather | solution.py:46
  70.4 2.3 copy.29
  72.7 80.0 %all-gather.6.cloned.1.call-done = bf16[2048,1024]{1,0:T(8,128)(2,1)} async-done(((bf16[512,1024]{1,0:T(8,128)(2,1)}), bf16[2048,1024]{1,0:T(8,128)(2,1)}) %all-gather.6.cloned.1.call-update) | async-done | bytes 4194320 | tf_op jit(solution)/shard_map/all_gather | solution.py:44
  152.7 6.4 %copy.27 = bf16[1024,2048]{1,0:T(8,128)(2,1)} copy(bf16[1024,2048]{0,1:T(8,128)(2,1)} %bitcast.14) | data formatting | bytes 8388608
  159.2 74.3 %all-gather.12.cloned.1.call-done = bf16[1024,2048]{1,0:T(8,128)(2,1)} async-done(((bf16[1024,512]{1,0:T(8,128)(2,1)}), bf16[1024,2048]{1,0:T(8,128)(2,1)}) %all-gather.12.cloned.1.call-update) | async-done | bytes 4194320 | tf_op jit(solution)/shard_map/all_gather | solution.py:47
  233.4 6.4 %copy.30 = bf16[2048,1024]{1,0:T(8,128)(2,1)} copy(bf16[2048,1024]{0,1:T(8,128)(2,1)} %bitcast.15) | data formatting | bytes 8388608
  (13 shorter events, 0.1 us)
Async XLA Ops:
  7.2 4.2 %copy-start = (bf16[16,1024]{1,0:T(8,128)(2,1)S(1)}, bf16[16,1024]{1,0:T(8,128)(2,1)}, u32[]{:S(2)}) copy-start(bf16[16,1024]{1,0:T(8,128)(2,1)} %param.16) | copy-start | bytes 98308
  7.2 33.7 %all-gather.8.cloned.1.call-start = ((), (), s32[]{:S(2)}) async-start(), calls=%async_computation.1 | async-start | bytes 1310720 | tf_op jit(solution)/shard_map/all_gather | solution.py:45
  9.2 4.9 %copy-start.1 = (bf16[1024,512]{1,0:T(8,128)(2,1)S(1)}, bf16[1024,512]{1,0:T(8,128)(2,1)}, u32[]{:S(2)}) copy-start(bf16[1024,512]{1,0:T(8,128)(2,1)} %param.23) | copy-start | bytes 3145732
  9.2 4.9 %copy-start.2 = (bf16[1024,16]{0,1:T(8,128)(2,1)S(1)}, bf16[1024,16]{0,1:T(8,128)(2,1)}, u32[]{:S(2)}) copy-start(bf16[1024,16]{0,1:T(8,128)(2,1)} %param.24) | copy-start | bytes 98308
  9.2 5.0 %copy-start.3 = (bf16[16,512]{1,0:T(8,128)(2,1)S(1)}, bf16[16,512]{1,0:T(8,128)(2,1)}, u32[]{:S(2)}) copy-start(bf16[16,512]{1,0:T(8,128)(2,1)} %param.25) | copy-start | bytes 49156
  9.2 61.2 %all-gather.10.cloned.1.call-start = ((), (), s32[]{:S(2)}) async-start(), calls=%async_computation.2 | async-start | bytes 1310720 | tf_op jit(solution)/shard_map/all_gather | solution.py:46
  11.3 141.4 %all-gather.6.cloned.1.call-start = ((), (), s32[]{:S(2)}) async-start(), calls=%async_computation | async-start | bytes 5242880 | tf_op jit(solution)/shard_map/all_gather | solution.py:44
  14.0 1.6 copy-start.4
  14.0 1.6 copy-start.5
  14.1 219.4 %all-gather.12.cloned.1.call-start = ((), (), s32[]{:S(2)}) async-start(), calls=%async_computation.3 | async-start | bytes 5242880 | tf_op jit(solution)/shard_map/all_gather | solution.py:47
Sparse Core Ops, SparseCore 0:
  10.1 30.7 all-gather.7
  43.0 27.3 all-gather.9
  72.6 80.1 all-gather.5
  154.2 79.2 all-gather.11
where the time goes:
time: 247 us; the launch traced here: 246 us
  waiting for transfers between devices  193 us (78%)
  local copies, waits for them, and re-layouts  18 us (7%)
  between operations  13.8 us (6%)
  blocking collectives  13.7 us (6%)
  matrix products  8.09 us (3%)
    all_gather x1, waiting for transfers between devices, on_device(): lax.all_gather(narrow_query, 'shard', axis=0, tiled=True)  80 us
    all_gather x1, waiting for transfers between devices, on_device(): lax.all_gather(narrow_mixed, 'shard', axis=1, tiled=True)  74.3 us
    all_gather x1, waiting for transfers between devices, on_device(): lax.all_gather(narrow_value, 'shard', axis=0, tiled=True)  27.3 us
    unnamed x18, local copies, waits for them, and re-layouts  18 us
    all_gather x1, blocking collectives, on_device(): lax.all_gather((norm_train + norm_step).astype(jnp.bfloat16), ('shard', '...  13.7 us
    all_gather x1, waiting for transfers between devices, on_device(): lax.all_gather(narrow_key, 'shard', axis=0, tiled=True)  10.9 us
  transfers between devices with their start and end apart: 4, of which 4 were waited for; matrix products, arithmetic and copies ran while one was open for 7% of the time, Pallas kernels for 0%

commit v1 on v0

v1 whole, which is shorter than its diff:
```python
import functools

import jax
import jax.numpy as jnp
from jax import lax
from jax.experimental import pallas as pl
from jax.experimental.pallas import tpu as pltpu
from jax.sharding import PartitionSpec as P

mix_rate = 0.5
MESH = pl.DeviceIdType.MESH
LANES = 128
SUBLANES = 8


def plain(
    w_query,
    low_query,
    high_query,
    w_key,
    low_key,
    high_key,
    w_value,
    low_value,
    high_value,
    w_mixed,
    low_mixed,
    high_mixed,
    norm_train,
    norm_step,
):
    def merged(w, low, high):
        low_rank = jnp.dot(low, high, preferred_element_type=jnp.float32)
        return (w.astype(jnp.float32) + mix_rate * low_rank).astype(jnp.bfloat16)

    query = lax.all_gather(merged(w_query, low_query, high_query), "shard", axis=0, tiled=True)
    key = lax.all_gather(merged(w_key, low_key, high_key), "shard", axis=0, tiled=True)
    value = lax.all_gather(merged(w_value, low_value, high_value), "shard", axis=0, tiled=True)
    mixed = lax.all_gather(merged(w_mixed, low_mixed, high_mixed), "shard", axis=1, tiled=True)
    norm = lax.all_gather(
        (norm_train + norm_step).astype(jnp.bfloat16), ("shard", "width"), axis=0, tiled=True
    )
    return query.T, key.T, value.T, mixed.T, norm


def kernel(
    n,
    given,
    train_ref,
    step_ref,
    outs,
    norm_out,
    copied,
    load_sem,
    send_sem,
    back_sem,
    recv_sem,
    pair_sem,
):
    me = lax.axis_index("shard")
    core = lax.axis_index("width")
    has_left, has_right = me > 0, me < n - 1
    left, right = {"shard": me - 1}, {"shard": me + 1}
    partner = {"width": 1 - core}

    loads = [
        pltpu.make_async_copy(source, copy, load_sem.at[i])
        for i, (source, copy) in enumerate(zip(given, copied))
    ]
    held, low_refs, high_refs = copied[0::3], copied[1::3], copied[2::3]
    for load in loads:
        load.start()

    barrier = pltpu.get_barrier_semaphore()
    pl.semaphore_signal(barrier, inc=1, device_id=partner, device_id_type=MESH)

    @pl.when(has_left)
    def _():
        pl.semaphore_signal(barrier, inc=1, device_id=left, device_id_type=MESH)

    @pl.when(has_right)
    def _():
        pl.semaphore_signal(barrier, inc=1, device_id=right, device_id_type=MESH)

    def piece(array, c, origin):
        if array == len(outs):
            return norm_out.at[origin]
        out, w = outs[array], held[array]
        if array < len(outs) - 1:
            block = w.shape[0]
            start = pl.multiple_of(origin * block, LANES)
            return out.at[pl.ds(pl.multiple_of(c * LANES, LANES), LANES), pl.ds(start, block)]
        start = pl.multiple_of(origin * w.shape[1] + c * LANES, LANES)
        return out.at[pl.ds(start, LANES)]

    counts = [w.shape[1] // LANES for w in held] + [1]
    firsts = [sum(counts[:i]) for i in range(len(counts))]

    def forward(array, c, origin):
        slot = firsts[array] + c
        return pltpu.make_async_remote_copy(
            src_ref=piece(array, c, origin),
            dst_ref=piece(array, c, origin),
            send_sem=send_sem.at[origin, slot],
            recv_sem=recv_sem.at[origin, slot],
            device_id=right,
            device_id_type=MESH,
        )

    def backward(array, c, origin, own=False):
        slot = firsts[array] + c
        return pltpu.make_async_remote_copy(
            src_ref=piece(array, c, origin),
            dst_ref=piece(array, c, origin),
            send_sem=back_sem.at[slot] if own else send_sem.at[origin, slot],
            recv_sem=recv_sem.at[origin, slot],
            device_id=left,
            device_id_type=MESH,
        )

    def compute(array, c):
        columns = pl.ds(pl.multiple_of(c * LANES, LANES), LANES)
        low_rank = lax.dot_general(
            high_refs[array][:, columns],
            low_refs[array][...],
            (((0,), (0,)), ((), ())),
            preferred_element_type=jnp.float32,
        )
        base = held[array][:, columns].astype(jnp.float32).T
        piece(array, c, me)[...] = (base + mix_rate * low_rank).astype(jnp.bfloat16)

    def send(array, c):
        @pl.when(has_right)
        def _():
            forward(array, c, me).start()

        @pl.when(has_left)
        def _():
            backward(array, c, me, own=True).start()

    norm_out[me, core] = train_ref[...] + step_ref[...]
    for load in loads[:3]:
        load.wait()
    compute(0, 0)

    pl.semaphore_wait(barrier, 1 + has_left.astype(jnp.int32) + has_right.astype(jnp.int32))

    pair = pltpu.make_async_remote_copy(
        src_ref=norm_out.at[me, core],
        dst_ref=norm_out.at[me, core],
        send_sem=pair_sem.at[0],
        recv_sem=pair_sem.at[1],
        device_id=partner,
        device_id_type=MESH,
    )
    pair.start()

    for array in range(len(outs)):
        if array:
            for load in loads[3 * array : 3 * array + 3]:
                load.wait()
            compute(array, 0)
            send(array - 1, counts[array - 1] - 1)

        def step(c, carry, array=array):
            compute(array, c)
            send(array, c - 1)
            return carry

        lax.fori_loop(1, counts[array], step, 0)
    pair.wait_send()
    pltpu.make_async_remote_copy(
        src_ref=norm_out.at[me, 1 - core],
        dst_ref=norm_out.at[me, 1 - core],
        send_sem=pair_sem.at[0],
        recv_sem=pair_sem.at[1],
        device_id=partner,
        device_id_type=MESH,
    ).wait_recv()
    send(len(outs) - 1, counts[len(outs) - 1] - 1)
    send(len(outs), 0)

    for k in range(1, n):
        from_left, from_right = me - k, me + k
        for array in range(len(counts)):

            def relay(c, carry, array=array, from_left=from_left, from_right=from_right):
                @pl.when(from_left >= 0)
                def _():
                    forward(array, c, from_left).wait_recv()

                    @pl.when(has_right)
                    def _():
                        forward(array, c, from_left).start()

                @pl.when(from_right < n)
                def _():
                    backward(array, c, from_right).wait_recv()

                    @pl.when(has_left)
                    def _():
                        backward(array, c, from_right).start()

                return carry

            lax.fori_loop(0, counts[array], relay, 0)

    for array in range(len(counts)):

        def drain(c, carry, array=array):
            @pl.when(has_right)
            def _():
                forward(array, c, me).wait_send()

            @pl.when(has_left)
            def _():
                backward(array, c, me, own=True).wait_send()

            for k in range(1, n):

                @pl.when(jnp.logical_and(me - k >= 0, has_right))
                def _(k=k):
                    forward(array, c, me - k).wait_send()

                @pl.when(jnp.logical_and(me + k < n, has_left))
                def _(k=k):
                    backward(array, c, me + k).wait_send()

            return carry

        lax.fori_loop(0, counts[array], drain, 0)


def body(n, *refs):
    kernel(n, refs[:12], refs[12], refs[13], refs[14:18], refs[18], refs[19:31], *refs[31:])


def on_device(n, cores, *args):
    weights, (norm_train, norm_step) = list(args[:12]), args[12:]
    bases = weights[0::3]
    whole_tiles = cores == 2 and all(size % LANES == 0 for w in bases for size in w.shape)
    if not whole_tiles:
        return plain(*args)
    (size,) = norm_train.shape
    tile = SUBLANES * LANES
    rows = -(-size // tile) * SUBLANES
    padding = rows * LANES - size

    def tiled(norm):
        return jnp.pad(norm, (0, padding)).reshape(rows, LANES)

    shapes = [(w.shape[1], w.shape[0] * n) for w in bases[:3]]
    shapes.append((bases[3].shape[1] * n, bases[3].shape[0]))
    slots = sum(w.shape[1] // LANES for w in bases) + 1
    weights[1::3] = [low.T for low in weights[1::3]]
    weights = [pltpu.with_memory_space_constraint(w, pltpu.HBM) for w in weights]
    in_hbm = pl.BlockSpec(memory_space=pltpu.HBM)
    in_vmem = pl.BlockSpec(memory_space=pltpu.VMEM)
    *finals, norm = pl.pallas_call(
        functools.partial(body, n),
        out_shape=[pltpu.VMEM(shape, jnp.bfloat16) for shape in shapes]
        + [pltpu.VMEM((n, cores, rows, LANES), jnp.float32)],
        in_specs=[in_hbm] * 12 + [in_vmem] * 2,
        out_specs=[in_vmem] * 5,
        scratch_shapes=[pltpu.VMEM(w.shape, w.dtype) for w in weights]
        + [
            pltpu.SemaphoreType.DMA((12,)),
            pltpu.SemaphoreType.DMA((n, slots)),
            pltpu.SemaphoreType.DMA((slots,)),
            pltpu.SemaphoreType.DMA((n, slots)),
            pltpu.SemaphoreType.DMA((2,)),
        ],
        compiler_params=pltpu.CompilerParams(
            collective_id=0, has_side_effects=True, vmem_limit_bytes=40 * 2**20
        ),
        name="merge_gather",
    )(*weights, tiled(norm_train), tiled(norm_step))
    serve_norm = norm.reshape(n * cores, rows * LANES)[:, :size].reshape(-1).astype(jnp.bfloat16)
    return (*finals, serve_norm)


def solution(mesh):
    placed = (
        P(("shift", "shard"), "width"),
        P(("shift", "shard"), None),
        P("shift", "width"),
        P(("shift", "shard"), "width"),
        P(("shift", "shard"), None),
        P("shift", "width"),
        P(("shift", "shard"), "width"),
        P(("shift", "shard"), None),
        P("shift", "width"),
        P(("shift", "width"), "shard"),
        P(("shift", "width"), None),
        P("shift", "shard"),
        P(("shift", "shard", "width")),
        P(("shift", "shard", "width")),
    )
    return jax.shard_map(
        functools.partial(on_device, mesh.shape["shard"], mesh.shape["width"]),
        mesh=mesh,
        in_specs=placed,
        out_specs=(
            P(("shift", "width"), None),
            P(("shift", "width"), None),
            P(("shift", "width"), None),
            P("shift", "width"),
            P("shift"),
        ),
        check_vma=False,
    )
```

time: 247 us -> 184 us (0.74)
  waiting for transfers between devices: 193 us -> 0 us
  Pallas kernels: 0 us -> 176 us
  blocking collectives: 13.7 us -> 0 us
  between operations: 13.8 us -> 0.65 us
  local copies, waits for them, and re-layouts: 18 us -> 7.28 us
  matrix products: 8.09 us -> 0 us
    all_gather x4 -> x0, waiting for transfers between devices: 192 us -> none  [the longest x1 80 us: on_device(): lax.all_gather(narrow_query, 'shard', axis=0, tiled=True)]
    pallas_call x0 -> x1, Pallas kernels: none -> 176 us  [on_device(): pl.pallas_call(functools.partial(body, n), out_shape=[pltpu.VMEM(shape, j...]
    all_gather x1 -> x0, blocking collectives: 13.7 us -> none  [on_device(): lax.all_gather((norm_train + norm_step).astype(jnp.bfloat16), ('shard', '...]
    unnamed x18 -> x7, local copies, waits for them, and re-layouts: 18 us -> 6.58 us
    dot_general x4 -> x0, matrix products: 8.09 us -> none  [the longest x1 2.67 us: on_device(): jnp.dot(low_query, high_query, preferred_element_type=jnp.float32)]
  transfers between devices with their start and end apart: 4 -> 0, of which waited for: 4 -> 0; matrix products, arithmetic and copies ran while one was open for 7% -> 0% of each run, Pallas kernels for 0% -> 0%
where the time goes in v1:
time: 184 us
  Pallas kernels  176 us (96%)
  local copies, waits for them, and re-layouts  7.28 us (4%)
    pallas_call x1, Pallas kernels, on_device(): pl.pallas_call(functools.partial(body, n), out_shape=[pltpu.VMEM(shape, j...  176 us
    unnamed x7, local copies, waits for them, and re-layouts  6.58 us

profile of v1, /device:TPU:0, one launch (start us, length us, event | category | flops | bytes accessed | tf_op | source)
XLA Modules:
  0.0 184.1 jit_solution(16921987267376217137)
XLA Ops:
  0.6 0.7 pad_bitcast_fusion
  1.3 176.2 %merge_gather.1 = (bf16[1024,2048]{1,0:T(8,128)(2,1)S(1)}, bf16[256,2048]{1,0:T(8,128)(2,1)S(1)}, bf16[256,2048]{1,0:T(8,128)(2,1)S(1)}, bf16[2048,1024]{1,0:T(8,128)(2,1)S(1)}, f32[4,2,8,128]{3,2,1,0:T(8,128)S(1)}) custom-call(bf16[512,1024]{1,0:T(8,128)(2,1)} %refs_0_.1, bf16[16,512]{1,0:T(8,128)(2,1)} %bitcast.19, bf16[16,1024]{1,0:T(8,128)(2,1)} %refs_2_.1, ...), custom_call_target="tpu_custom_call" | custom-call | tf_op jit(solution)/shard_map/merge_gather/pallas_call | solution.py:259
  177.5 2.0 %copy.27 = bf16[1024,2048]{1,0:T(8,128)(2,1)} copy(bf16[1024,2048]{1,0:T(8,128)(2,1)S(1)} %get-tuple-element.17) | data formatting | bytes 8388608
  179.5 0.6 copy.20
  180.1 1.0 copy.28
  181.1 1.0 copy.29
  182.1 2.0 %copy.30 = bf16[2048,1024]{1,0:T(8,128)(2,1)} copy(bf16[2048,1024]{1,0:T(8,128)(2,1)S(1)} %get-tuple-element.20) | data formatting | bytes 8388608
  (3 shorter events, 0.0 us)

commit v2 on v1

--- a/solution.py
+++ b/solution.py
@@ -10,7 +10,9 @@
 mix_rate = 0.5
 MESH = pl.DeviceIdType.MESH
 LANES = 128
-SUBLANES = 8
+COPY_ROWS = 256
+LATE_STEPS = 8
+LATE_PIECES = 2
 
 
 def plain(
@@ -43,11 +45,13 @@
     return query.T, key.T, value.T, mixed.T, norm
 
 
+def late_pieces(block):
+    return min(LATE_PIECES, block // LANES)
+
+
 def kernel(
     n,
     given,
-    train_ref,
-    step_ref,
     outs,
     norm_out,
     copied,
@@ -63,12 +67,21 @@
     left, right = {"shard": me - 1}, {"shard": me + 1}
     partner = {"width": 1 - core}
 
-    loads = [
-        pltpu.make_async_copy(source, copy, load_sem.at[i])
-        for i, (source, copy) in enumerate(zip(given, copied))
+    held, low_refs, high_refs = copied[0:12:3], copied[1:12:3], copied[2:12:3]
+    width = held[0].shape[1]
+    first, rest = pl.ds(0, LANES), pl.ds(LANES, width - LANES)
+    loads = [pltpu.make_async_copy(given[0].at[:, first], held[0].at[:, first], load_sem.at[0])]
+    loads += [
+        pltpu.make_async_copy(given[i], copied[i], load_sem.at[i]) for i in range(1, len(given))
     ]
-    held, low_refs, high_refs = copied[0::3], copied[1::3], copied[2::3]
-    for load in loads:
+    others = []
+    if width > LANES:
+        others.append(
+            pltpu.make_async_copy(
+                given[0].at[:, rest], held[0].at[:, rest], load_sem.at[len(loads)]
+            )
+        )
+    for load in loads[:3] + others + loads[3:]:
         load.start()
 
     barrier = pltpu.get_barrier_semaphore()
@@ -94,6 +107,9 @@
         return out.at[pl.ds(start, LANES)]
 
     counts = [w.shape[1] // LANES for w in held] + [1]
+    kept = counts[len(outs) - 1] - late_pieces(held[-1].shape[1])
+    moved = list(counts)
+    moved[len(outs) - 1] = jnp.where(core == 0, kept, counts[len(outs) - 1])
     firsts = [sum(counts[:i]) for i in range(len(counts))]
 
     def forward(array, c, origin):
@@ -130,37 +146,42 @@
         piece(array, c, me)[...] = (base + mix_rate * low_rank).astype(jnp.bfloat16)
 
     def send(array, c):
-        @pl.when(has_right)
+        ready = c < moved[array]
+
+        @pl.when(jnp.logical_and(has_right, ready))
         def _():
             forward(array, c, me).start()
 
-        @pl.when(has_left)
+        @pl.when(jnp.logical_and(has_left, ready))
         def _():
             backward(array, c, me, own=True).start()
 
-    norm_out[me, core] = train_ref[...] + step_ref[...]
     for load in loads[:3]:
         load.wait()
     compute(0, 0)
 
     pl.semaphore_wait(barrier, 1 + has_left.astype(jnp.int32) + has_right.astype(jnp.int32))
 
-    pair = pltpu.make_async_remote_copy(
-        src_ref=norm_out.at[me, core],
-        dst_ref=norm_out.at[me, core],
-        send_sem=pair_sem.at[0],
-        recv_sem=pair_sem.at[1],
-        device_id=partner,
-        device_id_type=MESH,
-    )
-    pair.start()
+    def exchange(side):
+        return pltpu.make_async_remote_copy(
+            src_ref=norm_out.at[me, side],
+            dst_ref=norm_out.at[me, side],
+            send_sem=pair_sem.at[0],
+            recv_sem=pair_sem.at[1],
+            device_id=partner,
+            device_id_type=MESH,
+        )
 
     for array in range(len(outs)):
+        for load in loads[3 * array : 3 * array + 3] if array else others:
+            load.wait()
         if array:
-            for load in loads[3 * array : 3 * array + 3]:
-                load.wait()
             compute(array, 0)
             send(array - 1, counts[array - 1] - 1)
+        if array == 1:
+            for load in loads[12:]:
+                load.wait()
+            norm_out[me, core] = copied[12][...] + copied[13][...]
 
         def step(c, carry, array=array):
             compute(array, c)
@@ -168,16 +189,12 @@
             return carry
 
         lax.fori_loop(1, counts[array], step, 0)
-    pair.wait_send()
-    pltpu.make_async_remote_copy(
-        src_ref=norm_out.at[me, 1 - core],
-        dst_ref=norm_out.at[me, 1 - core],
-        send_sem=pair_sem.at[0],
-        recv_sem=pair_sem.at[1],
-        device_id=partner,
-        device_id_type=MESH,
-    ).wait_recv()
+    exchange(core).start()
+
     send(len(outs) - 1, counts[len(outs) - 1] - 1)
+
+    exchange(core).wait_send()
+    exchange(1 - core).wait_recv()
     send(len(outs), 0)
 
     for k in range(1, n):
@@ -203,7 +220,7 @@
 
                 return carry
 
-            lax.fori_loop(0, counts[array], relay, 0)
+            lax.fori_loop(0, moved[array], relay, 0)
 
     for array in range(len(counts)):
 
@@ -228,43 +245,197 @@
 
             return carry
 
-        lax.fori_loop(0, counts[array], drain, 0)
+        lax.fori_loop(0, moved[array], drain, 0)
 
 
 def body(n, *refs):
-    kernel(n, refs[:12], refs[12], refs[13], refs[14:18], refs[18], refs[19:31], *refs[31:])
+    kernel(n, refs[:14], refs[14:18], refs[18], refs[19:33], *refs[33:])
+
+
+def store(n, cores, *refs):
+    gathered, norm_ref, outs, norm_out, flat, sem, mixed_sem = refs[:4], refs[4], refs[5:9], *refs[9:]
+    me, core = lax.axis_index("shard"), lax.axis_index("width")
+    copies = []
+    for source, out in zip(gathered[:3], outs[:3]):
+        for row in range(0, source.shape[0], COPY_ROWS):
+            rows = pl.ds(row, min(COPY_ROWS, source.shape[0] - row))
+            copies.append(
+                pltpu.make_async_copy(source.at[rows], out.at[rows], sem.at[len(copies)])
+            )
+
+    block = gathered[3].shape[0] // n
+    tail = late_pieces(block) * LANES
+
+    def mixed(origin, row, size, part):
+        rows = pl.ds(origin * block + row, size)
+        return pltpu.make_async_copy(
+            gathered[3].at[rows], outs[3].at[rows], mixed_sem.at[origin, part]
+        )
+
+    if block > tail:
+        copies += [mixed(origin, 0, block - tail, 0) for origin in range(n)]
+
+    def each_last(act):
+        for origin in range(n):
+
+            @pl.when(jnp.logical_or(core != 0, me == origin))
+            def _(origin=origin):
+                act(mixed(origin, block - tail, tail, 1))
+
+    for copy in copies:
+        copy.start()
+    each_last(lambda copy: copy.start())
+    rows = norm_ref.shape[2]
+    for origin in range(n):
+        for side in range(cores):
+            flat[pl.ds((origin * cores + side) * rows, rows)] = norm_ref[origin, side]
+    norm_out[...] = flat[...].astype(norm_out.dtype)
+    for copy in copies:
+        copy.wait()
+    each_last(lambda copy: copy.wait())
+
+
+def late(n, mixed, after, out, send_sem, back_sem, recv_sem):
+    me = lax.axis_index("shard")
+    core = lax.axis_index("width")
+    has_left, has_right = me > 0, me < n - 1
+    left, right = {"shard": me - 1}, {"shard": me + 1}
+    block = mixed.shape[0] // n
+    tail = late_pieces(block) * LANES
+    size = tail // LATE_STEPS
+
+    def copy(origin, step, device, semaphore, own):
+        rows = pl.ds(pl.multiple_of(step * size, size), size)
+        first = pl.multiple_of(me * block + block - tail + step * size, size)
+        return pltpu.make_async_remote_copy(
+            src_ref=mixed.at[pl.ds(first, size)] if own else out.at[origin, rows],
+            dst_ref=out.at[origin, rows],
+            send_sem=semaphore,
+            recv_sem=recv_sem.at[origin, step],
+            device_id=device,
+            device_id_type=MESH,
+        )
+
+    def forward(origin, step, own=False):
+        return copy(origin, step, right, send_sem.at[origin, step], own)
+
+    def backward(origin, step, own=False):
+        semaphore = back_sem.at[step] if own else send_sem.at[origin, step]
+        return copy(origin, step, left, semaphore, own)
+
+    @pl.when(core == 0)
+    def _():
+        barrier = pltpu.get_barrier_semaphore()
+
+        @pl.when(has_left)
+        def _():
+            pl.semaphore_signal(barrier, inc=1, device_id=left, device_id_type=MESH)
+
+        @pl.when(has_right)
+        def _():
+            pl.semaphore_signal(barrier, inc=1, device_id=right, device_id_type=MESH)
+
+        pl.semaphore_wait(barrier, has_left.astype(jnp.int32) + has_right.astype(jnp.int32))
+
+        for step in range(LATE_STEPS):
+
+            @pl.when(has_right)
+            def _(step=step):
+                forward(me, step, own=True).start()
+
+            @pl.when(has_left)
+            def _(step=step):
+                backward(me, step, own=True).start()
+
+        for k in range(1, n):
+
+            def relay(step, carry, k=k):
+                @pl.when(me - k >= 0)
+                def _():
+                    forward(me - k, step).wait_recv()
+
+                    @pl.when(has_right)
+                    def _():
+                        forward(me - k, step).start()
+
+                @pl.when(me + k < n)
+                def _():
+                    backward(me + k, step).wait_recv()
+
+                    @pl.when(has_left)
+                    def _():
+                        backward(me + k, step).start()
+
+                return carry
+
+            lax.fori_loop(0, LATE_STEPS, relay, 0)
+
+        def drain(step, carry):
+            @pl.when(has_right)
+            def _():
+                forward(me, step, own=True).wait_send()
+
+            @pl.when(has_left)
+            def _():
+                backward(me, step, own=True).wait_send()
+
+            for k in range(1, n):
+
+                @pl.when(jnp.logical_and(me - k >= 0, has_right))
+                def _(k=k):
+                    forward(me - k, step).wait_send()
+
+                @pl.when(jnp.logical_and(me + k < n, has_left))
+                def _(k=k):
+                    backward(me + k, step).wait_send()
+
+            return carry
+
+        lax.fori_loop(0, LATE_STEPS, drain, 0)
+
+
+def store_late(n, pieces, given, out, sem):
+    me, core = lax.axis_index("shard"), lax.axis_index("width")
+    block = out.shape[0] // n
+    tail = late_pieces(block) * LANES
+
+    def each(act):
+        for origin in range(n):
+
+            @pl.when(jnp.logical_and(core == 0, me != origin))
+            def _(origin=origin):
+                rows = pl.ds((origin + 1) * block - tail, tail)
+                act(pltpu.make_async_copy(pieces.at[origin], out.at[rows], sem.at[origin]))
+
+    each(lambda copy: copy.start())
+    each(lambda copy: copy.wait())
 
 
 def on_device(n, cores, *args):
     weights, (norm_train, norm_step) = list(args[:12]), args[12:]
     bases = weights[0::3]
-    whole_tiles = cores == 2 and all(size % LANES == 0 for w in bases for size in w.shape)
-    if not whole_tiles:
+    (size,) = norm_train.shape
+    sizes = [size, *(size for w in bases for size in w.shape)]
+    if cores != 2 or any(size % LANES for size in sizes):
         return plain(*args)
-    (size,) = norm_train.shape
-    tile = SUBLANES * LANES
-    rows = -(-size // tile) * SUBLANES
-    padding = rows * LANES - size
-
-    def tiled(norm):
-        return jnp.pad(norm, (0, padding)).reshape(rows, LANES)
-
+    rows = size // LANES
     shapes = [(w.shape[1], w.shape[0] * n) for w in bases[:3]]
     shapes.append((bases[3].shape[1] * n, bases[3].shape[0]))
     slots = sum(w.shape[1] // LANES for w in bases) + 1
-    weights[1::3] = [low.T for low in weights[1::3]]
-    weights = [pltpu.with_memory_space_constraint(w, pltpu.HBM) for w in weights]
     in_hbm = pl.BlockSpec(memory_space=pltpu.HBM)
     in_vmem = pl.BlockSpec(memory_space=pltpu.VMEM)
-    *finals, norm = pl.pallas_call(
+    weights[1::3] = [low.T for low in weights[1::3]]
+    norms = [norm_train.reshape(rows, LANES), norm_step.reshape(rows, LANES)]
+    given = [pltpu.with_memory_space_constraint(array, pltpu.HBM) for array in weights + norms]
+    gathered = pl.pallas_call(
         functools.partial(body, n),
         out_shape=[pltpu.VMEM(shape, jnp.bfloat16) for shape in shapes]
         + [pltpu.VMEM((n, cores, rows, LANES), jnp.float32)],
-        in_specs=[in_hbm] * 12 + [in_vmem] * 2,
+        in_specs=[in_hbm] * 14,
         out_specs=[in_vmem] * 5,
-        scratch_shapes=[pltpu.VMEM(w.shape, w.dtype) for w in weights]
+        scratch_shapes=[pltpu.VMEM(array.shape, array.dtype) for array in given]
         + [
-            pltpu.SemaphoreType.DMA((12,)),
+            pltpu.SemaphoreType.DMA((15,)),
             pltpu.SemaphoreType.DMA((n, slots)),
             pltpu.SemaphoreType.DMA((slots,)),
             pltpu.SemaphoreType.DMA((n, slots)),
@@ -274,9 +445,50 @@
             collective_id=0, has_side_effects=True, vmem_limit_bytes=40 * 2**20
         ),
         name="merge_gather",
-    )(*weights, tiled(norm_train), tiled(norm_step))
-    serve_norm = norm.reshape(n * cores, rows * LANES)[:, :size].reshape(-1).astype(jnp.bfloat16)
-    return (*finals, serve_norm)
+    )(*given)
+    norm_rows = n * cores * rows
+    *finals, norm = pl.pallas_call(
+        functools.partial(store, n, cores),
+        out_shape=[jax.ShapeDtypeStruct(shape, jnp.bfloat16) for shape in shapes]
+        + [jax.ShapeDtypeStruct((norm_rows, LANES), jnp.bfloat16)],
+        in_specs=[in_vmem] * 5,
+        out_specs=[in_hbm] * 4 + [in_vmem],
+        scratch_shapes=[
+            pltpu.VMEM((norm_rows, LANES), jnp.float32),
+            pltpu.SemaphoreType.DMA((sum(-(-shape[0] // COPY_ROWS) for shape in shapes[:3]),)),
+            pltpu.SemaphoreType.DMA((n, 2)),
+        ],
+        compiler_params=pltpu.CompilerParams(vmem_limit_bytes=20 * 2**20),
+        name="store",
+    )(*gathered)
+    columns = shapes[3][1]
+    tail = late_pieces(bases[3].shape[1]) * LANES
+    pieces = pl.pallas_call(
+        functools.partial(late, n),
+        out_shape=pltpu.VMEM((n, tail, columns), jnp.bfloat16),
+        in_specs=[in_vmem, in_hbm],
+        out_specs=in_vmem,
+        scratch_shapes=[
+            pltpu.SemaphoreType.DMA((n, LATE_STEPS)),
+            pltpu.SemaphoreType.DMA((LATE_STEPS,)),
+            pltpu.SemaphoreType.DMA((n, LATE_STEPS)),
+        ],
+        compiler_params=pltpu.CompilerParams(
+            collective_id=1, has_side_effects=True, vmem_limit_bytes=20 * 2**20
+        ),
+        name="late",
+    )(gathered[3], pltpu.with_memory_space_constraint(finals[3], pltpu.HBM))
+    finals[3] = pl.pallas_call(
+        functools.partial(store_late, n),
+        out_shape=jax.ShapeDtypeStruct(shapes[3], jnp.bfloat16),
+        in_specs=[in_vmem, in_hbm],
+        out_specs=in_hbm,
+        input_output_aliases={1: 0},
+        scratch_shapes=[pltpu.SemaphoreType.DMA((n,))],
+        compiler_params=pltpu.CompilerParams(vmem_limit_bytes=20 * 2**20),
+        name="store_late",
+    )(pieces, finals[3])
+    return (*finals, norm.reshape(-1))
 
 
 def solution(mesh):

time: 184 us -> 177 us (0.962)
  local copies, waits for them, and re-layouts: 7.28 us -> 0 us
    pallas_call x1, Pallas kernels: 176 us -> 143 us  [on_device(): pl.pallas_call(functools.partial(body, n), out_shape=[pltpu.VMEM(shape, j...]
    pallas_call x0 -> x3, Pallas kernels: none -> 32.7 us  [the longest x1 27.3 us: on_device(): pl.pallas_call(functools.partial(late, n), out_shape=pltpu.VMEM((n, tail,...]
    unnamed x7 -> x0, local copies, waits for them, and re-layouts: 6.58 us -> none
where the time goes in v2:
time: 177 us; the launch traced here: 176 us
  Pallas kernels  176 us (99%)
    pallas_call x1, Pallas kernels, on_device(): pl.pallas_call(functools.partial(body, n), out_shape=[pltpu.VMEM(shape, j...  143 us
    pallas_call x1, Pallas kernels, on_device(): pl.pallas_call(functools.partial(late, n), out_shape=pltpu.VMEM((n, tail,...  27.3 us
    pallas_call x1, Pallas kernels, on_device(): pl.pallas_call(functools.partial(store, n, cores), out_shape=[jax.ShapeDt...  4.18 us

profile of v2, /device:TPU:0, one launch (start us, length us, event | category | flops | bytes accessed | tf_op | source)
XLA Modules:
  0.0 176.5 jit_solution(899462857314307816)
XLA Ops:
  0.6 143.1 %merge_gather.1 = (bf16[1024,2048]{1,0:T(8,128)(2,1)S(1)}, bf16[256,2048]{1,0:T(8,128)(2,1)S(1)}, bf16[256,2048]{1,0:T(8,128)(2,1)S(1)}, bf16[2048,1024]{1,0:T(8,128)(2,1)S(1)}, f32[4,2,2,128]{3,2,1,0:T(2,128)S(1)}) custom-call(bf16[512,1024]{1,0:T(8,128)(2,1)} %refs_0_.1, bf16[16,512]{1,0:T(8,128)(2,1)} %bitcast.8, bf16[16,1024]{1,0:T(8,128)(2,1)} %refs_2_.1, ...), custom_call_target="tpu_custom_call" | custom-call | tf_op jit(solution)/shard_map/merge_gather/pallas_call | solution.py:430
  143.8 4.2 %store.1 = (bf16[1024,2048]{1,0:T(8,128)(2,1)}, bf16[256,2048]{1,0:T(8,128)(2,1)}, bf16[256,2048]{1,0:T(8,128)(2,1)}, bf16[2048,1024]{1,0:T(8,128)(2,1)}, bf16[16,128]{1,0:T(8,128)(2,1)}) custom-call(bf16[1024,2048]{1,0:T(8,128)(2,1)S(1)} %get-tuple-element.15.refs_0_, bf16[256,2048]{1,0:T(8,128)(2,1)S(1)} %get-tuple-element.16.refs_1_, ...), custom_call_target="tpu_custom_call" | custom-call | tf_op jit(solution)/shard_map/store/pallas_call | solution.py:450
  147.9 27.3 %late.1.pieces = bf16[4,256,1024]{2,1,0:T(8,128)(2,1)S(1)} custom-call(bf16[2048,1024]{1,0:T(8,128)(2,1)S(1)} %get-tuple-element.18.refs_3_.mixed, bf16[2048,1024]{1,0:T(8,128)(2,1)} %get-tuple-element.23.after.given), custom_call_target="tpu_custom_call" | custom-call | tf_op jit(solution)/shard_map/late/pallas_call | solution.py:466
  175.3 1.2 store_late.1
